TPU v7x, 256 devices: a whole 4x4x8 slice. The times are simulated.
256 devices in a mesh: sims: 4 (over z_hi, core), blk: 64 (over x, z_lo, y).
Axes of the slice: x: 4, y: 4, z: 8 (z_hi: 2, z_lo: 4; z = z_hi * 4 + z_lo), core: 2. Of those that a mesh axis runs over, the one named last changes fastest.
Arguments:
- sim_alm: bfloat16 [1536, 16, 2, 1536], P('blk', 'sims'), may hold values from -6 to 6
- t_filter: float32 [1536], replicated, may hold values from 0.0006510417 to 0.00390625
- wiener_filter: float32 [1536], replicated, may hold values from 8.477105e-07 to 5.086263e-06
- colatitude: float32 [128], replicated, may hold values from 1.09712 to 1.60288, as said below
- legendre: bfloat16 [1536, 1536, 128], P('blk'), may hold values from -2 to 2, as said below
- pixel_mask: int32 [128, 4096], P('blk'), may hold values 0 or 1
Outputs:
- field_sum: float32 [1536, 2, 1536], P('blk', None, 'sims')
- spectra: float32 [16, 2, 1536], P('sims')
Inputs may be any that keep to these rules, and one draw needn't show every extreme that they name: `colatitude`: the colatitudes of 128 cycles in increasing order, about 0.0016 apart, in a band centred between 1.2 and 1.5. legendre[m,l,r] is the orthonormal associated Legendre function of degree l and order m at colatitude[r], zero for l < m, rounded to bfloat16.
All inputs are finite; a program needn't handle non-finite values. No bound on the sum of `pixel_mask` on one device may be relied on, other than what follows from the above.
Results may differ from a plain program's by a relative error of at most 0.006.
The roundings to bfloat16 on the way count: a program that leaves them out, or rounds other values in their place, can miss the bound.
Values may be sent and summed in bfloat16 or wider, within the bound.
No kernel may reach another device: no remote copies, remote signals or barrier semaphores. Data moves between devices by JAX's collectives and lax.ppermute only.
A program may use at most 192 MiB of HBM per device.

v0:
```python
import math
import jax
import jax.numpy as jnp
from jax import lax
from jax.sharding import Mesh
from jax.sharding import PartitionSpec as P

BLK = ("blk_0", "blk_1", "blk_2")


def in_blocks(shard, dim, length):
    before, after = (shard.shape[:dim], shard.shape[dim + 1 :])
    return jnp.moveaxis(shard.reshape(*before, length, -1, *after), dim, 0)


def in_order(pieces, dim):
    pieces = jnp.moveaxis(pieces, 0, dim)
    dims = pieces.shape
    return pieces.reshape(*dims[:dim], dims[dim] * dims[dim + 1], *dims[dim + 2 :])


def exchange_in_order(pieces, axes, turns):
    inside = pieces.shape[1:]
    result = pieces.reshape(*(lax.axis_size(a) for a in axes), *inside)
    for k in turns:
        result = lax.all_to_all(result, axes[k], k, k, tiled=True)
    return result.reshape(-1, *inside)


def exchange_by_axis(shard, axes, turns, split_dim, concat_dim):
    pieces = in_blocks(shard, split_dim, lax.axis_size(axes))
    return in_order(exchange_in_order(pieces, axes, turns), concat_dim)


def from_everyone(shard, axis):
    length = lax.axis_size(axis)
    return lax.all_to_all(
        jnp.broadcast_to(shard[None], (length, *shard.shape)), axis, 0, 0, tiled=True
    )


def taken_together(shard, axis):
    everything = from_everyone(shard, axis)
    return jnp.sum(everything.astype(jnp.float32), axis=0)


def ladder(degree, orders):
    numerator = (2.0 * degree + 1.0) * (degree * degree - orders * orders)
    denominator = jnp.maximum(2.0 * degree - 1.0, 1.0)
    return jnp.where(degree > orders, jnp.sqrt(jnp.maximum(numerator, 0.0) / denominator), 0.0)


def fourier_table(mode_count, pixels):
    mode_ids = jnp.arange(mode_count, dtype=jnp.int32)[:, None]
    pixel_ids = jnp.arange(pixels, dtype=jnp.int32)[None, :]
    phases = 2.0 * math.pi / pixels * (mode_ids * pixel_ids % pixels).astype(jnp.float32)
    return jnp.stack(
        [jnp.cos(phases).astype(jnp.bfloat16), (-jnp.sin(phases)).astype(jnp.bfloat16)], axis=1
    )


def per_device(sim_alm, t_filter, wiener_filter, colatitude, legendre, pixel_mask):
    local_modes = sim_alm.shape[0]
    sims_here = sim_alm.shape[1]
    degrees = sim_alm.shape[3]
    cycle_count = legendre.shape[2]
    pixels = pixel_mask.shape[1]
    blocks = lax.axis_size(BLK)
    cycle_local = cycle_count // blocks
    first_mode = lax.axis_index(BLK) * local_modes
    degree = jnp.arange(degrees, dtype=jnp.float32)
    local_orders = (first_mode + jnp.arange(local_modes, dtype=jnp.int32)).astype(jnp.float32)
    all_orders = jnp.arange(degrees, dtype=jnp.float32)
    ladder_steps = ladder(degree[None, :], local_orders[:, None])
    cotangent = jnp.cos(colatitude) / jnp.sin(colatitude)
    cosecant = 1.0 / jnp.sin(colatitude)
    tilt_grid = jnp.cos(colatitude).reshape(blocks, 1, cycle_local)
    values = sim_alm.astype(jnp.float32)
    weighted = wiener_filter * values
    raised = ladder_steps[:, None, None, :] * weighted
    lowered = jnp.concatenate([raised[..., 1:], jnp.zeros_like(raised[..., :1])], axis=-1)
    coefs = jnp.stack([t_filter * values, weighted, degree * weighted, lowered], axis=1).astype(
        jnp.bfloat16
    )
    flattened = coefs.reshape(local_modes, 8 * sims_here, degrees)
    legsum = jnp.einsum("mkl,mlr->krm", flattened, legendre, preferred_element_type=jnp.float32)
    legsum = legsum.reshape(4, sims_here, 2, cycle_count, local_modes)
    rotated = jnp.stack([-legsum[1][:, 1], legsum[1][:, 0]], axis=1) * (
        cosecant[:, None] * local_orders[None, :]
    )
    slopes = cotangent[:, None] * legsum[2] - cosecant[:, None] * legsum[3]
    cycle_coefs = jnp.stack([legsum[0], rotated, slopes], axis=0).astype(jnp.bfloat16)
    cycle_coefs = cycle_coefs.reshape(3, sims_here, 2, cycle_count * local_modes)
    fourier = fourier_table(degrees, pixels)
    fourier_grid = fourier.reshape(blocks, local_modes, 2, pixels)
    mode_weight = (
        jnp.where(all_orders > 0, 2.0, 1.0).astype(jnp.bfloat16).reshape(blocks, 1, local_modes)
    )
    pixel_weight = pixel_mask.astype(jnp.float32)
    legendre_grid = legendre.reshape(local_modes, degrees, blocks, cycle_local)
    arranged = lax.all_to_all(cycle_coefs, BLK, split_axis=3, concat_axis=3, tiled=True).reshape(
        3, -1, 2, blocks, cycle_local, local_modes
    )
    scaled = arranged * mode_weight
    cycle_maps = jnp.einsum(
        "qscbrn,bncj->qsrj", scaled, fourier_grid, preferred_element_type=jnp.float32
    )
    product = pixel_weight * cycle_maps[0]
    flow_maps = jnp.stack([product * cycle_maps[2], product * cycle_maps[1]]).astype(jnp.bfloat16)
    mode_coefs = jnp.einsum(
        "psrj,mcj->pscmr", flow_maps, fourier, preferred_element_type=jnp.float32
    )
    mode_coefs = (mode_coefs * (2.0 * math.pi / pixels)).astype(jnp.bfloat16)
    mode_coefs = mode_coefs.reshape(2, mode_coefs.shape[1], 2, degrees * cycle_local)
    returned = exchange_by_axis(mode_coefs, BLK, (0, 1, 2), 3, 3)
    returned = returned.reshape(2, -1, 2, blocks, local_modes, cycle_local)
    tilted = (tilt_grid * returned[0].astype(jnp.float32)).astype(jnp.bfloat16)
    stacked = jnp.stack([tilted, returned[0], returned[1]], axis=0)
    projected = jnp.einsum(
        "kscbnr,nlbr->knscl", stacked, legendre_grid, preferred_element_type=jnp.float32
    )
    shifted = jnp.concatenate(
        [jnp.zeros_like(projected[1][..., :1]), projected[1][..., :-1]], axis=-1
    )
    first_part = projected[0]
    third_part = projected[2]
    order_column = local_orders[:, None, None]
    step_rows = ladder_steps[:, None, :]
    real_part = (
        degree * first_part[:, :, 0]
        - step_rows * shifted[:, :, 0]
        + order_column * third_part[:, :, 1]
    )
    imag_part = (
        degree * first_part[:, :, 1]
        - step_rows * shifted[:, :, 1]
        - order_column * third_part[:, :, 0]
    )
    estimates = jnp.stack([real_part, imag_part], axis=2) / degrees
    partial_value = jnp.sum(estimates, axis=1)
    quarter = degrees // lax.axis_size("sims")
    field_total = taken_together(partial_value.astype(jnp.bfloat16), "sims").astype(jnp.float32)
    field_share = lax.dynamic_slice_in_dim(
        field_total, lax.axis_index("sims") * quarter, quarter, 2
    )
    sim_total = sims_here * lax.axis_size("sims")
    residual = estimates - field_total[:, None] / sim_total
    partner = residual.reshape(local_modes, sims_here // 2, 2, 2, degrees)[:, :, ::-1].reshape(
        residual.shape
    )
    auto_power = jnp.sum(residual * residual, axis=2)
    cross_power = jnp.sum(residual * partner, axis=2)
    local_weight = jnp.where(local_orders > 0, 2.0, 1.0)
    local_power = jnp.stack(
        [
            jnp.einsum("m,msl->sl", local_weight, auto_power),
            jnp.einsum("m,msl->sl", local_weight, cross_power),
        ],
        axis=1,
    )
    summed = taken_together(local_power.astype(jnp.bfloat16), BLK).astype(jnp.float32)
    spectra = summed / (2.0 * degree + 1.0)
    return (field_share, spectra)


def solution(mesh):
    torus = Mesh(
        mesh.devices.reshape(mesh.shape["sims"], 4, 4, 4), ("sims", "blk_0", "blk_1", "blk_2")
    )
    return jax.shard_map(
        per_device,
        mesh=torus,
        in_specs=(P(BLK, "sims", None, None), P(), P(), P(), P(BLK, None, None), P(BLK, None)),
        out_specs=(P(BLK, None, "sims"), P("sims", None, None)),
        check_vma=False,
    )
```

profile of v0, /device:TPU:1, one launch (start us, length us, event | category | flops | bytes accessed | tf_op | source)
XLA Modules:
  0.0 460.9 jit_solution(1568018498141478940)
XLA Ops:
  0.9 0.5 copy-done
  1.4 2.4 convert_bitcast_fusion
  3.8 1.3 fusion.24
  5.1 0.5 pad_bitcast_fusion
  5.6 4.6 pad_maximum_fusion
  10.2 3.9 copy.204
  14.0 5.0 %convert_element_type.158 = bf16[24,32,1536]{2,1,0:T(8,128)(2,1)S(1)} reshape(bf16[24,4,4,2,1536]{4,3,2,1,0:T(2,128)(2,1)} %copy.204) | data formatting | bytes 4718592 | tf_op jit(solution)/shard_map/convert_element_type | solution.py:82
  19.0 4.6 %convolution_bitcast_fusion = f32[32,128,24]{1,0,2:T(8,128)S(1)} fusion(bf16[24,32,1536]{2,1,0:T(8,128)(2,1)S(1)} %convert_element_type.158, bf16[24,1536,128]{2,1,0:T(8,128)(2,1)} %param.10), kind=kOutput, calls=%fused_computation.37 | convolution fusion | flops 301989888 | bytes 12189696 | tf_op jit(solution)/shard_map/mkl,mlr->krm/dot_general | solution.py:86
  24.7 0.5 copy-done.5
  27.7 8.1 %copy.212 = bf16[3,4,2,3072]{1,2,0,3:T(2,128)(2,1)} copy(bf16[3,4,2,3072]{3,2,1,0:T(2,128)(2,1)S(1)} %pad_maximum_fusion.1) | data formatting | bytes 294912 | tf_op jit(solution)/shard_map/stack | solution.py:92
  35.7 12.9 %reshape.533 = bf16[64,2,576]{2,1,0:T(2,128)(2,1)} reshape(bf16[3072,3,2,4]{3,2,1,0:T(2,128)(2,1)} %bitcast.120) | data formatting | bytes 294912
  48.6 12.5 %all-to-all-start = ((bf16[64,2,576]{2,1,0:T(2,128)(2,1)}), bf16[64,2,576]{2,1,0:T(2,128)(2,1)S(1)}, u32[]{:S(2)}, u32[]{:S(2)}) async-start(bf16[64,2,576]{2,1,0:T(2,128)(2,1)} %reshape.533), calls=%async_computation | async-start | bytes 327680 | tf_op jit(solution)/shard_map/all_to_all | solution.py:101
  61.1 101.2 %negate_convert_fusion.1 = (bf16[1536,1,4096]{2,0,1:T(8,128)(2,1)}, bf16[1536,1,4096]{2,0,1:T(8,128)(2,1)}) fusion(), kind=kLoop, calls=%fused_computation.18 | loop fusion | flops 106954752 | bytes 25165824 | tf_op jit(solution)/shard_map/convert_element_type | solution.py:58
  162.4 104.7 %cosine_convert_fusion = (bf16[64,24,1,4096]{3,0,1,2:T(8,128)(2,1)}, bf16[64,24,1,4096]{3,0,1,2:T(8,128)(2,1)}) fusion(s32[64,24]{0,1:T(8,128)S(1)} %multiply_add_fusion), kind=kLoop, calls=%fused_computation.15 | loop fusion | flops 106954752 | bytes 25171968 | tf_op jit(solution)/shard_map/convert_element_type | solution.py:58
  267.1 6.4 %reshape.534 = bf16[3072,3,2,4]{3,2,1,0:T(2,128)(2,1)} reshape(bf16[64,2,576]{2,1,0:T(2,128)(2,1)S(1)} %all-to-all-done) | data formatting | bytes 294912
  273.5 11.2 %copy.243 = bf16[3,4,2,64,2,24]{5,4,3,2,1,0:T(2,128)(2,1)S(1)} copy(bf16[3,4,2,64,2,24]{1,2,0,5,4,3:T(2,128)(2,1)} %bitcast.121) | data formatting | bytes 294912 | tf_op jit(solution)/shard_map/reshape | solution.py:101
  284.7 0.7 broadcast_multiply_fusion
  285.4 0.7 copy.214
  286.1 10.3 %fusion.16 = f32[3,4,2,4096]{3,1,2,0:T(4,128)S(1)} fusion(bf16[3,4,2,64,2,24]{3,1,5,2,4,0:T(4,128)(2,1)S(1)} %copy.214, bf16[64,24,1,4096]{3,0,1,2:T(8,128)(2,1)} %get-tuple-element.29, bf16[64,24,1,4096]{3,0,1,2:T(8,128)(2,1)} %get-tuple-element.28), kind=kOutput, calls=%fused_computation.28 | convolution fusion | flops 616562688 | bytes 25706496 | tf_op jit(solution)/shard_map/qscbrn,bncj->qsrj/dot_general | solution.py:105
  296.5 11.8 %fusion.22 = bf16[2,4,2,1536,2]{3,1,4,0,2:T(4,128)(2,1)S(1)} fusion(bf16[1536,1,4096]{2,0,1:T(8,128)(2,1)} %get-tuple-element.36, bf16[1536,1,4096]{2,0,1:T(8,128)(2,1)} %get-tuple-element.37, bf16[1,4,2,4096]{3,1,2,0:T(4,128)(2,1)S(1)} %get-tuple-element.20, bf16[1,4,2,4096]{3,1,2,0:T(4,128)(2,1)S(1)} %get-tuple-element.19), kind=kOutput, calls=%fused_computation.34 | convolution fusion | flops 453345280 | bytes 25395200 | tf_op jit(solution)/shard_map/psrj,mcj->pscmr/dot_general | solution.py:110
  308.2 2.8 copy.215
  311.0 2.4 copy.216
  313.4 0.4 reshape.535
  313.8 8.3 %all_to_all.30 = bf16[4,2,6144]{2,1,0:T(2,128)(2,1)S(1)} all-to-all(bf16[4,2,6144]{2,1,0:T(2,128)(2,1)S(1)} %reshape.535), channel_id=1, replica_groups=mesh['sims'=4,'blk_0'=4,'blk_1'=4,'blk_2'=4] {'blk_0'}, dimensions={0} | all-to-all | bytes 196608 | tf_op jit(solution)/shard_map/all_to_all | solution.py:26
  322.8 8.8 %all_to_all.31 = bf16[4,2,6144]{2,1,0:T(2,128)(2,1)S(1)} all-to-all(bf16[4,2,6144]{2,1,0:T(2,128)(2,1)S(1)} %reshape.537), channel_id=1, replica_groups=mesh['sims'=4,'blk_0'=4,'blk_1'=4,'blk_2'=4] {'blk_1'}, dimensions={0} | all-to-all | bytes 196608 | tf_op jit(solution)/shard_map/all_to_all | solution.py:26
  332.1 1.0 reshape.539
  333.1 4.0 all-to-all-start.3
  337.1 0.8 mul.379
  337.9 13.1 %copy.225 = bf16[24,1536,128]{1,0,2:T(8,128)(2,1)} copy(bf16[24,1536,128]{2,1,0:T(8,128)(2,1)} %param.10) | data formatting | bytes 18874368 | tf_op args[4]
  352.1 14.7 %fusion.17 = f32[3,24,4,2,1536]{4,2,3,0,1:T(4,128)S(1)} fusion(bf16[24,1536,64,2,1,1]{1,0,3,2,5,4:T(8,128)(2,1)} %bitcast.119, bf16[1,4,2,64,24,2]{3,1,5,2,0,4:T(4,128)(2,1)S(1)} %copy.224, bf16[1,4,2,64,24,2]{3,1,5,2,0,4:T(4,128)(2,1)S(1)} %copy.221, bf16[1,4,2,64,24,2]{3,1,5,2,0,4:T(4,128)(2,1)S(1)} %multiply_convert_fusion.1), kind=kOutput, calls=%fused_computation.29 | convolution fusion | flops 226934784 | bytes 13123584 | tf_op jit(solution)/shard_map/kscbnr,nlbr->knscl/dot_general | solution.py:119
  366.8 0.8 slice_bitcast_fusion.2
  367.7 0.8 fusion.29
  368.5 1.0 fusion.26
  369.6 0.9 broadcast_in_dim.22
  370.4 10.1 %all-to-all-start.4 = ((bf16[4,24,2,1536]{3,1,2,0:T(8,128)(2,1)}), bf16[4,24,2,1536]{3,1,2,0:T(8,128)(2,1)S(1)}, u32[]{:S(2)}, u32[]{:S(2)}) async-start(bf16[4,24,2,1536]{3,1,2,0:T(8,128)(2,1)} %broadcast_in_dim.22), calls=%async_computation.4 | async-start | bytes 1179648 | tf_op jit(solution)/shard_map/all_to_all | solution.py:37
  380.6 0.5 stack.88
  381.0 0.5 stack.89
  381.5 13.2 %all-to-all-done.4 = bf16[4,24,2,1536]{3,1,2,0:T(8,128)(2,1)S(1)} async-done(((bf16[4,24,2,1536]{3,1,2,0:T(8,128)(2,1)}), bf16[4,24,2,1536]{3,1,2,0:T(8,128)(2,1)S(1)}, u32[]{:S(2)}, u32[]{:S(2)}) %all-to-all-start.4) | async-done | bytes 589856 | tf_op jit(solution)/shard_map/all_to_all | solution.py:37
  395.1 0.6 multiply_reduce_fusion.1
  395.9 1.9 fusion.25
  397.9 7.0 %rev.3 = f32[24,2,2,2,1536]{4,2,1,0,3:T(2,128)S(1)} reverse(f32[24,2,2,2,1536]{4,2,1,0,3:T(2,128)} %fusion.25), dimensions={2} | reverse | bytes 2359296 | tf_op jit(solution)/shard_map/rev | solution.py:148
  404.9 1.4 multiply_reduce_fusion
  406.6 2.0 broadcast_in_dim.25
  408.6 11.7 %all-to-all-start.5 = ((bf16[64,4,2,1536]{3,2,1,0:T(2,128)(2,1)}), bf16[64,4,2,1536]{3,2,1,0:T(2,128)(2,1)S(1)}, u32[]{:S(2)}, u32[]{:S(2)}) async-start(bf16[64,4,2,1536]{3,2,1,0:T(2,128)(2,1)} %broadcast_in_dim.25), calls=%async_computation.5 | async-start | bytes 3145728 | tf_op jit(solution)/shard_map/all_to_all | solution.py:37
  420.3 0.7 copy.233
  421.0 38.5 %all-to-all-done.5 = bf16[64,4,2,1536]{3,2,1,0:T(2,128)(2,1)S(1)} async-done(((bf16[64,4,2,1536]{3,2,1,0:T(2,128)(2,1)}), bf16[64,4,2,1536]{3,2,1,0:T(2,128)(2,1)S(1)}, u32[]{:S(2)}, u32[]{:S(2)}) %all-to-all-start.5) | async-done | bytes 1572896 | tf_op jit(solution)/shard_map/all_to_all | solution.py:37
  459.5 0.5 convert_reduce_fusion
  460.0 0.6 broadcast_divide_fusion
  (76 shorter events, 6.8 us)
Async XLA Ops:
  0.7 23.9 %copy-start.3 = (f32[24]{0:T(128)}, f32[24]{0:T(128)S(1)}, u32[]{:S(2)}) copy-start(f32[24]{0:T(128)S(1)} %add_convert_fusion) | copy-start | bytes 292
  0.7 0.6 copy-start
  19.0 5.6 %copy-start.6 = (f32[128]{0:T(128)S(1)}, f32[128]{0:T(128)}, u32[]{:S(2)}) copy-start(f32[128]{0:T(128)} %param.9) | copy-start | bytes 1540
  24.7 0.5 copy-start.5
  48.6 218.5 %all-to-all-start = ((bf16[64,2,576]{2,1,0:T(2,128)(2,1)}), bf16[64,2,576]{2,1,0:T(2,128)(2,1)S(1)}, u32[]{:S(2)}, u32[]{:S(2)}) async-start(bf16[64,2,576]{2,1,0:T(2,128)(2,1)} %reshape.533), calls=%async_computation | async-start | bytes 327680 | tf_op jit(solution)/shard_map/all_to_all | solution.py:101
  162.4 104.7 %copy-start.2 = (s32[2,4096]{1,0:T(2,128)S(1)}, s32[2,4096]{1,0:T(2,128)}, u32[]{:S(2)}) copy-start(s32[2,4096]{1,0:T(2,128)} %param.11) | copy-start | bytes 98308
  333.1 17.9 %all-to-all-start.3 = ((bf16[4,2,6144]{2,1,0:T(2,128)(2,1)}), bf16[4,2,6144]{2,1,0:T(2,128)(2,1)S(1)}, u32[]{:S(2)}, u32[]{:S(2)}) async-start(bf16[4,2,6144]{2,1,0:T(2,128)(2,1)} %reshape.539), calls=%async_computation.3 | async-start | bytes 196608 | tf_op jit(solution)/shard_map/all_to_all | solution.py:26
  366.8 0.9 copy-start.4
  370.4 24.3 %all-to-all-start.4 = ((bf16[4,24,2,1536]{3,1,2,0:T(8,128)(2,1)}), bf16[4,24,2,1536]{3,1,2,0:T(8,128)(2,1)S(1)}, u32[]{:S(2)}, u32[]{:S(2)}) async-start(bf16[4,24,2,1536]{3,1,2,0:T(8,128)(2,1)} %broadcast_in_dim.22), calls=%async_computation.4 | async-start | bytes 1179648 | tf_op jit(solution)/shard_map/all_to_all | solution.py:37
  397.9 62.1 %copy-start.1 = (f32[1536]{0:T(1024)S(1)}, f32[1536]{0:T(1024)}, u32[]{:S(2)}) copy-start(f32[1536]{0:T(1024)} %copy-done) | copy-start | bytes 18436
  408.6 50.8 %all-to-all-start.5 = ((bf16[64,4,2,1536]{3,2,1,0:T(2,128)(2,1)}), bf16[64,4,2,1536]{3,2,1,0:T(2,128)(2,1)S(1)}, u32[]{:S(2)}, u32[]{:S(2)}) async-start(bf16[64,4,2,1536]{3,2,1,0:T(2,128)(2,1)} %broadcast_in_dim.25), calls=%async_computation.5 | async-start | bytes 3145728 | tf_op jit(solution)/shard_map/all_to_all | solution.py:37
where the time goes:
time: 465 us; the launch traced here: 461 us
  other arithmetic  223 us (48%)
  local copies, waits for them, and re-layouts  87.7 us (19%)
  waiting for transfers between devices  51.7 us (11%)
  matrix products  41.8 us (9%)
  starting transfers between devices  38.3 us (8%)
  blocking collectives  17.2 us (4%)
    convert_element_type x1, other arithmetic, fourier_table(): jnp.cos(phases).astype(jnp.bfloat16)  105 us
    convert_element_type x1, other arithmetic, fourier_table(): (-jnp.sin(phases)).astype(jnp.bfloat16)  101 us
    all_to_all x2, waiting for transfers between devices, from_everyone(): lax.all_to_all(jnp.broadcast_to(shard[None], (length, *shard.shape)), axi...  51.7 us
    unnamed x27, local copies, waits for them, and re-layouts  36.9 us
    all_to_all x2, starting transfers between devices, from_everyone(): lax.all_to_all(jnp.broadcast_to(shard[None], (length, *shard.shape)), axi...  21.8 us
    all_to_all x2, blocking collectives, exchange_in_order(): result = lax.all_to_all(result, axes[k], k, k, tiled=True)  17.2 us
    dot_general x1, matrix products, per_device(): jnp.einsum('kscbnr,nlbr->knscl', stacked, legendre_grid, preferred_elemen...  14.7 us
    all_to_all x1, starting transfers between devices, per_device(): lax.all_to_all(cycle_coefs, BLK, split_axis=3, concat_axis=3, tiled=True)  12.5 us
  transfers between devices with their start and end apart: 4, of which 2 were waited for; matrix products, arithmetic and copies ran while one was open for 48% of the time, Pallas kernels for 0%

commit v1 on v0

--- a/solution.py
+++ b/solution.py
@@ -6,6 +6,15 @@
 from jax.sharding import PartitionSpec as P
 
 BLK = ("blk_0", "blk_1", "blk_2")
+form_sites = lambda a_name, mine_x: jnp.concatenate(
+    lax.all_to_all(
+        jnp.stack(jnp.split(mine_x, lax.axis_size(a_name), axis=3)),
+        a_name,
+        split_axis=0,
+        concat_axis=0,
+    ),
+    3,
+)
 
 
 def in_blocks(shard, dim, length):
@@ -98,9 +107,7 @@
     )
     pixel_weight = pixel_mask.astype(jnp.float32)
     legendre_grid = legendre.reshape(local_modes, degrees, blocks, cycle_local)
-    arranged = lax.all_to_all(cycle_coefs, BLK, split_axis=3, concat_axis=3, tiled=True).reshape(
-        3, -1, 2, blocks, cycle_local, local_modes
-    )
+    arranged = form_sites(BLK, cycle_coefs).reshape(3, -1, 2, blocks, cycle_local, local_modes)
     scaled = arranged * mode_weight
     cycle_maps = jnp.einsum(
         "qscbrn,bncj->qsrj", scaled, fourier_grid, preferred_element_type=jnp.float32

time: 465 us -> 433 us (0.931)
  local copies, waits for them, and re-layouts: 87.7 us -> 55.9 us
    unnamed x27 -> x90, local copies, waits for them, and re-layouts: 36.9 us -> 24.4 us
    reshape x1, local copies, waits for them, and re-layouts: 11.2 us -> 0.49 us  [jnp.concatenate(lax.all_to_all(jnp.stack(jnp.split(mine_x, lax.axis_size(...]
    another operation x2 -> x1, local copies, waits for them, and re-layouts: 8.4 us -> 0.34 us  [per_device(): jnp.stack([legsum[0], rotated, slopes], axis=0).astype(jnp.bfloat16)]
  transfers between devices with their start and end apart: 4 -> 4, of which waited for: 2 -> 2; matrix products, arithmetic and copies ran while one was open for 48% -> 52% of each run, Pallas kernels for 0% -> 0%
where the time goes in v1:
time: 433 us; the launch traced here: 429 us
  other arithmetic  222 us (51%)
  local copies, waits for them, and re-layouts  55.9 us (13%)
  waiting for transfers between devices  51.7 us (12%)
  matrix products  41.9 us (10%)
  starting transfers between devices  38.5 us (9%)
  blocking collectives  17.3 us (4%)
    convert_element_type x1, other arithmetic, fourier_table(): jnp.cos(phases).astype(jnp.bfloat16)  105 us
    convert_element_type x1, other arithmetic, fourier_table(): (-jnp.sin(phases)).astype(jnp.bfloat16)  101 us
    all_to_all x2, waiting for transfers between devices, from_everyone(): lax.all_to_all(jnp.broadcast_to(shard[None], (length, *shard.shape)), axi...  51.7 us
    unnamed x90, local copies, waits for them, and re-layouts  24.4 us
    all_to_all x2, starting transfers between devices, from_everyone(): lax.all_to_all(jnp.broadcast_to(shard[None], (length, *shard.shape)), axi...  21.8 us
    all_to_all x2, blocking collectives, exchange_in_order(): result = lax.all_to_all(result, axes[k], k, k, tiled=True)  17.3 us
    dot_general x1, matrix products, per_device(): jnp.einsum('kscbnr,nlbr->knscl', stacked, legendre_grid, preferred_elemen...  14.7 us
    all_to_all x1, starting transfers between devices, lax.all_to_all(jnp.stack(jnp.split(mine_x, lax.axis_size(a_name), axis=3)...  12.8 us
  transfers between devices with their start and end apart: 4, of which 2 were waited for; matrix products, arithmetic and copies ran while one was open for 52% of the time, Pallas kernels for 0%

profile of v1, /device:TPU:1, one launch (start us, length us, event | category | flops | bytes accessed | tf_op | source)
XLA Modules:
  0.0 428.8 jit_solution(13947730931923651965)
XLA Ops:
  0.9 0.5 copy-done
  1.4 2.4 convert_bitcast_fusion
  3.8 1.3 fusion.24
  5.1 0.5 pad_bitcast_fusion
  5.6 4.6 %pad_maximum_fusion = bf16[24,4,4,2,1536]{4,3,2,0,1:T(2,128)(2,1)S(1)} fusion(bf16[24,1,4,2,1536]{4,3,2,0,1:T(2,128)(2,1)S(1)} %pad_bitcast_fusion, bf16[24,1,4,2,1536]{4,3,2,0,1:T(2,128)(2,1)S(1)} %get-tuple-element.16, bf16[24,1,4,2,1536]{4,3,2,0,1:T(2,128)(2,1)S(1)} %get-tuple-element.15, bf16[24,1,4,2,1536]{4,3,2,0,1:T(2,128)(2,1)S(1)} %get-tuple-element.18), kind=kLoop, calls=%fused_computation.31 | loop fusion | flops 3538944 | bytes 4718592 | tf_op jit(solution)/shard_map/stack | solution.py:91
  10.2 3.9 copy.174
  14.0 5.0 %convert_element_type.158 = bf16[24,32,1536]{2,1,0:T(8,128)(2,1)S(1)} reshape(bf16[24,4,4,2,1536]{4,3,2,1,0:T(2,128)(2,1)} %copy.174) | data formatting | bytes 4718592 | tf_op jit(solution)/shard_map/convert_element_type | solution.py:91
  19.0 4.6 %convolution_bitcast_fusion = f32[32,128,24]{1,0,2:T(8,128)S(1)} fusion(bf16[24,32,1536]{2,1,0:T(8,128)(2,1)S(1)} %convert_element_type.158, bf16[24,1536,128]{2,1,0:T(8,128)(2,1)} %param.10), kind=kOutput, calls=%fused_computation.37 | convolution fusion | flops 301989888 | bytes 12189696 | tf_op jit(solution)/shard_map/mkl,mlr->krm/dot_general | solution.py:95
  24.7 0.5 copy-done.5
  26.9 0.3 stack.273
  32.6 1.3 reshape.533
  33.9 12.8 %all-to-all-start = ((bf16[64,2,576]{2,1,0:T(2,128)(2,1)}), bf16[64,2,576]{2,1,0:T(2,128)(2,1)S(1)}, u32[]{:S(2)}, u32[]{:S(2)}) async-start(bf16[64,2,576]{2,1,0:T(2,128)(2,1)} %reshape.533), calls=%async_computation | async-start | bytes 327680 | tf_op jit(solution)/shard_map/all_to_all | solution.py:10
  46.6 101.2 %negate_convert_fusion.1 = (bf16[1536,1,4096]{2,0,1:T(8,128)(2,1)}, bf16[1536,1,4096]{2,0,1:T(8,128)(2,1)}) fusion(), kind=kLoop, calls=%fused_computation.18 | loop fusion | flops 106954752 | bytes 25165824 | tf_op jit(solution)/shard_map/convert_element_type | solution.py:67
  147.9 104.7 %cosine_convert_fusion = (bf16[64,24,1,4096]{3,0,1,2:T(8,128)(2,1)}, bf16[64,24,1,4096]{3,0,1,2:T(8,128)(2,1)}) fusion(s32[64,24]{0,1:T(8,128)S(1)} %multiply_add_fusion), kind=kLoop, calls=%fused_computation.15 | loop fusion | flops 106954752 | bytes 25171968 | tf_op jit(solution)/shard_map/convert_element_type | solution.py:67
  252.6 0.5 reshape.534
  253.1 0.5 copy.182
  253.6 10.4 %fusion.16 = f32[3,4,2,4096]{3,1,2,0:T(4,128)S(1)} fusion(bf16[64,24,1,4096]{3,0,1,2:T(8,128)(2,1)} %get-tuple-element.29, bf16[64,24,1,4096]{3,0,1,2:T(8,128)(2,1)} %get-tuple-element.28, bf16[3,4,2,64,2,24]{3,5,4,2,1,0:T(8,128)(2,1)S(1)} %broadcast_multiply_fusion.1), kind=kOutput, calls=%fused_computation.28 | convolution fusion | flops 616562688 | bytes 25706496 | tf_op jit(solution)/shard_map/qscbrn,bncj->qsrj/dot_general | solution.py:112
  264.1 11.8 %fusion.22 = bf16[2,4,2,1536,2]{3,1,4,0,2:T(4,128)(2,1)S(1)} fusion(bf16[1536,1,4096]{2,0,1:T(8,128)(2,1)} %get-tuple-element.36, bf16[1536,1,4096]{2,0,1:T(8,128)(2,1)} %get-tuple-element.37, bf16[1,4,2,4096]{3,1,2,0:T(4,128)(2,1)S(1)} %get-tuple-element.20, bf16[1,4,2,4096]{3,1,2,0:T(4,128)(2,1)S(1)} %get-tuple-element.19), kind=kOutput, calls=%fused_computation.34 | convolution fusion | flops 453345280 | bytes 25395200 | tf_op jit(solution)/shard_map/psrj,mcj->pscmr/dot_general | solution.py:117
  275.9 2.8 copy.184
  278.6 2.4 copy.185
  281.0 0.4 reshape.535
  281.4 8.4 %all_to_all.30 = bf16[4,2,6144]{2,1,0:T(2,128)(2,1)S(1)} all-to-all(bf16[4,2,6144]{2,1,0:T(2,128)(2,1)S(1)} %reshape.535), channel_id=1, replica_groups=mesh['sims'=4,'blk_0'=4,'blk_1'=4,'blk_2'=4] {'blk_0'}, dimensions={0} | all-to-all | bytes 196608 | tf_op jit(solution)/shard_map/all_to_all | solution.py:35
  290.2 0.4 reshape.537
  290.6 8.8 %all_to_all.31 = bf16[4,2,6144]{2,1,0:T(2,128)(2,1)S(1)} all-to-all(bf16[4,2,6144]{2,1,0:T(2,128)(2,1)S(1)} %reshape.537), channel_id=1, replica_groups=mesh['sims'=4,'blk_0'=4,'blk_1'=4,'blk_2'=4] {'blk_1'}, dimensions={0} | all-to-all | bytes 196608 | tf_op jit(solution)/shard_map/all_to_all | solution.py:35
  299.9 1.0 reshape.539
  300.9 4.0 all-to-all-start.3
  304.9 0.8 mul.379
  305.7 13.3 %copy.194 = bf16[24,1536,128]{1,0,2:T(8,128)(2,1)} copy(bf16[24,1536,128]{2,1,0:T(8,128)(2,1)} %param.10) | data formatting | bytes 18874368 | tf_op args[4]
  319.3 0.3 copy.188
  320.1 14.7 %fusion.17 = f32[3,24,4,2,1536]{4,2,3,0,1:T(4,128)S(1)} fusion(bf16[24,1536,64,2,1,1]{1,0,3,2,5,4:T(8,128)(2,1)} %bitcast.373, bf16[1,4,2,64,24,2]{3,1,5,2,0,4:T(4,128)(2,1)S(1)} %copy.193, bf16[1,4,2,64,24,2]{3,1,5,2,0,4:T(4,128)(2,1)S(1)} %copy.190, bf16[1,4,2,64,24,2]{3,1,5,2,0,4:T(4,128)(2,1)S(1)} %multiply_convert_fusion.1), kind=kOutput, calls=%fused_computation.29 | convolution fusion | flops 226934784 | bytes 13123584 | tf_op jit(solution)/shard_map/kscbnr,nlbr->knscl/dot_general | solution.py:126
  334.8 0.8 slice_bitcast_fusion.2
  335.6 0.8 fusion.29
  336.5 1.0 fusion.26
  337.5 0.9 broadcast_in_dim.22
  338.4 10.1 %all-to-all-start.4 = ((bf16[4,24,2,1536]{3,1,2,0:T(8,128)(2,1)}), bf16[4,24,2,1536]{3,1,2,0:T(8,128)(2,1)S(1)}, u32[]{:S(2)}, u32[]{:S(2)}) async-start(bf16[4,24,2,1536]{3,1,2,0:T(8,128)(2,1)} %broadcast_in_dim.22), calls=%async_computation.4 | async-start | bytes 1179648 | tf_op jit(solution)/shard_map/all_to_all | solution.py:46
  348.5 0.5 stack.348
  349.0 0.5 stack.349
  349.5 13.2 %all-to-all-done.4 = bf16[4,24,2,1536]{3,1,2,0:T(8,128)(2,1)S(1)} async-done(((bf16[4,24,2,1536]{3,1,2,0:T(8,128)(2,1)}), bf16[4,24,2,1536]{3,1,2,0:T(8,128)(2,1)S(1)}, u32[]{:S(2)}, u32[]{:S(2)}) %all-to-all-start.4) | async-done | bytes 589856 | tf_op jit(solution)/shard_map/all_to_all | solution.py:46
  363.1 0.6 multiply_reduce_fusion.1
  363.9 1.9 fusion.25
  365.8 7.0 %rev.3 = f32[24,2,2,2,1536]{4,2,1,0,3:T(2,128)S(1)} reverse(f32[24,2,2,2,1536]{4,2,1,0,3:T(2,128)} %fusion.25), dimensions={2} | reverse | bytes 2359296 | tf_op jit(solution)/shard_map/rev | solution.py:155
  372.9 1.4 multiply_reduce_fusion
  374.6 2.0 broadcast_in_dim.25
  376.6 11.7 %all-to-all-start.5 = ((bf16[64,4,2,1536]{3,2,1,0:T(2,128)(2,1)}), bf16[64,4,2,1536]{3,2,1,0:T(2,128)(2,1)S(1)}, u32[]{:S(2)}, u32[]{:S(2)}) async-start(bf16[64,4,2,1536]{3,2,1,0:T(2,128)(2,1)} %broadcast_in_dim.25), calls=%async_computation.5 | async-start | bytes 3145728 | tf_op jit(solution)/shard_map/all_to_all | solution.py:46
  388.3 0.7 copy.202
  388.9 38.5 %all-to-all-done.5 = bf16[64,4,2,1536]{3,2,1,0:T(2,128)(2,1)S(1)} async-done(((bf16[64,4,2,1536]{3,2,1,0:T(2,128)(2,1)}), bf16[64,4,2,1536]{3,2,1,0:T(2,128)(2,1)S(1)}, u32[]{:S(2)}, u32[]{:S(2)}) %all-to-all-start.5) | async-done | bytes 1572896 | tf_op jit(solution)/shard_map/all_to_all | solution.py:46
  427.4 0.5 convert_reduce_fusion
  428.0 0.6 broadcast_divide_fusion
  (138 shorter events, 10.6 us)
Async XLA Ops:
  0.7 23.9 %copy-start.3 = (f32[24]{0:T(128)}, f32[24]{0:T(128)S(1)}, u32[]{:S(2)}) copy-start(f32[24]{0:T(128)S(1)} %add_convert_fusion) | copy-start | bytes 292
  0.7 0.6 copy-start
  19.0 5.6 %copy-start.6 = (f32[128]{0:T(128)S(1)}, f32[128]{0:T(128)}, u32[]{:S(2)}) copy-start(f32[128]{0:T(128)} %param.9) | copy-start | bytes 1540
  24.7 0.5 copy-start.5
  33.9 218.7 %all-to-all-start = ((bf16[64,2,576]{2,1,0:T(2,128)(2,1)}), bf16[64,2,576]{2,1,0:T(2,128)(2,1)S(1)}, u32[]{:S(2)}, u32[]{:S(2)}) async-start(bf16[64,2,576]{2,1,0:T(2,128)(2,1)} %reshape.533), calls=%async_computation | async-start | bytes 327680 | tf_op jit(solution)/shard_map/all_to_all | solution.py:10
  147.9 104.7 %copy-start.2 = (s32[2,4096]{1,0:T(2,128)S(1)}, s32[2,4096]{1,0:T(2,128)}, u32[]{:S(2)}) copy-start(s32[2,4096]{1,0:T(2,128)} %param.11) | copy-start | bytes 98308
  300.9 18.1 %all-to-all-start.3 = ((bf16[4,2,6144]{2,1,0:T(2,128)(2,1)}), bf16[4,2,6144]{2,1,0:T(2,128)(2,1)S(1)}, u32[]{:S(2)}, u32[]{:S(2)}) async-start(bf16[4,2,6144]{2,1,0:T(2,128)(2,1)} %reshape.539), calls=%async_computation.3 | async-start | bytes 196608 | tf_op jit(solution)/shard_map/all_to_all | solution.py:35
  334.8 0.9 copy-start.4
  338.4 24.3 %all-to-all-start.4 = ((bf16[4,24,2,1536]{3,1,2,0:T(8,128)(2,1)}), bf16[4,24,2,1536]{3,1,2,0:T(8,128)(2,1)S(1)}, u32[]{:S(2)}, u32[]{:S(2)}) async-start(bf16[4,24,2,1536]{3,1,2,0:T(8,128)(2,1)} %broadcast_in_dim.22), calls=%async_computation.4 | async-start | bytes 1179648 | tf_op jit(solution)/shard_map/all_to_all | solution.py:46
  365.8 62.1 %copy-start.1 = (f32[1536]{0:T(1024)S(1)}, f32[1536]{0:T(1024)}, u32[]{:S(2)}) copy-start(f32[1536]{0:T(1024)} %copy-done) | copy-start | bytes 18436
  376.6 50.8 %all-to-all-start.5 = ((bf16[64,4,2,1536]{3,2,1,0:T(2,128)(2,1)}), bf16[64,4,2,1536]{3,2,1,0:T(2,128)(2,1)S(1)}, u32[]{:S(2)}, u32[]{:S(2)}) async-start(bf16[64,4,2,1536]{3,2,1,0:T(2,128)(2,1)} %broadcast_in_dim.25), calls=%async_computation.5 | async-start | bytes 3145728 | tf_op jit(solution)/shard_map/all_to_all | solution.py:46
